TPU v7x, 32 devices: a whole 2x2x4 slice. The times are simulated.
32 devices in a mesh: group: 2 (over y), tp: 16 (over z, x, core).
Axes of the slice: x: 2, y: 2, z: 4, core: 2. Of those that a mesh axis runs over, the one named last changes fastest.
Arguments:
- queries: bfloat16 [2, 8, 2, 8192], P('group', None, None, 'tp'), may hold values from -24 to 24
- new_keys: bfloat16 [2, 8, 2, 1024], P('group', None, None, 'tp'), may hold values from -16 to 16
- new_values: bfloat16 [2, 8, 2, 1024], P('group', None, None, 'tp'), may hold values from -24 to 24
- key_pages: bfloat16 [2, 1024, 16, 1024], P('group', 'tp'), may hold values from -16 to 16
- value_pages: bfloat16 [2, 1024, 16, 1024], P('group', 'tp'), may hold values from -24 to 24
- page_owner: int32 [2, 1024], P('group', 'tp'), may hold values from 0 to 8, as said below
- page_fill: int32 [2, 1024], P('group', 'tp'), may hold values from 0 to 16, as said below
- target_slot: int32 [2, 8], P('group'), may hold values from 0 to 8, as said below
- out_weight: bfloat16 [8192, 8192], P(None, 'tp'), may hold values from -0.0625 to 0.0625
Outputs:
- projected: bfloat16 [2, 8, 2, 8192], P('group', None, None, 'tp')
Inputs may be any that keep to these rules, and one draw needn't show every extreme that they name: `page_owner`: the owning request slot, or 8 for a free page. Of each pair of groups g and g XOR (1) one is loaded (no free pages) and the other light; group 0 is light, and so is group 2 - 1 when 2 > 2. One device holds at most 16 pages of moving requests, and some device of every loaded group holds exactly 16. `page_fill`: 1 to 16 for a used page, 0 for a free one. `target_slot`: 8 for a request that stays. Every group has exactly one moving request; their slots in the partner group are distinct and own no pages there.
All inputs are finite; a program needn't handle non-finite values.
Results may differ from a plain program's by a relative error of at most 0.0065.
Values may be sent and summed in bfloat16 or wider, within the bound.
No kernel may reach another device: no remote copies, remote signals or barrier semaphores. Data moves between devices by JAX's collectives and lax.ppermute only.
A program may use at most 64 MiB of HBM per device.

v0:
```python
import math
import jax
import jax.numpy as jnp
from jax import lax
from jax.sharding import PartitionSpec as P

HEADS = 64
KVH = 8
HD = 128
PAGE = 16
MOVE = 1
neg_big = -1e30


def swapped(value, axis, distance):
    return lax.ppermute(value, axis, [(i, i ^ 1 << distance) for i in range(lax.axis_size(axis))])


def combined_all(part, axis, combine):
    gathered = jax.tree.map(lambda a: lax.all_gather(a, axis), part)

    def take(source):
        return jax.tree.map(lambda a: lax.dynamic_index_in_dim(a, source, 0, False), gathered)

    return lax.fori_loop(
        1, lax.axis_size(axis), lambda source, state: combine(state, take(source)), take(0)
    )


def merge_states(first, second):
    largest = jnp.maximum(first[0], second[0])
    scale_first = jnp.exp(first[0] - largest)
    scale_second = jnp.exp(second[0] - largest)
    return (
        largest,
        first[1] * scale_first + second[1] * scale_second,
        first[2] * scale_first[..., None] + second[2] * scale_second[..., None],
    )


def page_states(query_rows, key_block, value_block, owner_rows, fill_counts, row_count):
    page_count = key_block.shape[0]
    step_count = query_rows.shape[1]
    group_size = HEADS // KVH
    scale_factor = 1.0 / math.sqrt(HD)
    clipped = jnp.clip(owner_rows, 0, row_count - 1)
    query_page = jnp.take(query_rows, clipped, axis=0).reshape(
        page_count, step_count, KVH, group_size, HD
    )
    key_page = key_block.reshape(page_count, PAGE, KVH, HD)
    value_page = value_block.reshape(page_count, PAGE, KVH, HD)
    scores = (
        jnp.einsum("psgjd,ptgd->psgjt", query_page, key_page, preferred_element_type=jnp.float32)
        * scale_factor
    )
    live_token = (owner_rows < row_count)[:, None] & (
        lax.broadcasted_iota(jnp.int32, (page_count, PAGE), 1) < fill_counts[:, None]
    )
    token_mask = live_token[:, None, None, None, :]
    scores = jnp.where(token_mask, scores, neg_big)
    page_top = jnp.max(scores, axis=4).reshape(page_count, step_count * HEADS)
    member = owner_rows[None, :] == lax.broadcasted_iota(jnp.int32, (row_count, page_count), 0)
    row_top = jnp.max(jnp.where(member[:, :, None], page_top[None], neg_big), axis=1)
    top_page = jnp.take(row_top, clipped, axis=0).reshape(
        page_count, step_count, KVH, group_size, 1
    )
    weights = jnp.where(token_mask, jnp.exp(scores - top_page), 0.0).astype(jnp.bfloat16)
    weighted = jnp.einsum(
        "psgjt,ptgd->psgjd", weights, value_page, preferred_element_type=jnp.float32
    ).reshape(page_count, step_count * HEADS * HD)
    weight_sum = jnp.sum(weights.astype(jnp.float32), axis=4).reshape(
        page_count, step_count * HEADS
    )
    onehot = member.astype(jnp.float32)
    row_sum = jnp.dot(onehot, weight_sum, precision=lax.Precision.HIGHEST)
    row_acc = jnp.dot(onehot, weighted, precision=lax.Precision.HIGHEST)
    return (
        row_top.reshape(row_count, step_count, HEADS),
        row_sum.reshape(row_count, step_count, HEADS),
        row_acc.reshape(row_count, step_count, HEADS, HD),
    )


def new_token_states(query_heads, key_rows, value_rows, head_kv):
    row_count = key_rows.shape[0]
    step_count = key_rows.shape[1]
    scale_factor = 1.0 / math.sqrt(HD)
    key_heads = jnp.take(key_rows.reshape(row_count, step_count, KVH, HD), head_kv, axis=2)
    value_heads = jnp.take(
        value_rows.reshape(row_count, step_count, KVH, HD), head_kv, axis=2
    ).astype(jnp.float32)
    scores = (
        jnp.einsum("rshd,ruhd->rshu", query_heads, key_heads, preferred_element_type=jnp.float32)
        * scale_factor
    )
    causal = (
        lax.broadcasted_iota(jnp.int32, (step_count, step_count), 1)
        <= lax.broadcasted_iota(jnp.int32, (step_count, step_count), 0)
    )[None, :, None, :]
    scores = jnp.where(causal, scores, neg_big)
    largest = jnp.max(scores, axis=3)
    weights = jnp.where(causal, jnp.exp(scores - largest[..., None]), 0.0)
    return (
        largest,
        jnp.sum(weights, axis=3),
        jnp.einsum("rshu,ruhd->rshd", weights, value_heads, precision=lax.Precision.HIGHEST),
    )


def per_device(
    queries,
    new_keys,
    new_values,
    key_pages,
    value_pages,
    page_owner,
    page_fill,
    target_slot,
    out_weight,
):
    row_count = queries.shape[1]
    step_count = queries.shape[2]
    partner_bit = lax.axis_size("group").bit_length() - 2
    query_rows, key_rows, value_rows = (
        lax.all_gather(queries[0], "tp", axis=2, tiled=True),
        lax.all_gather(new_keys[0], "tp", axis=2, tiled=True),
        lax.all_gather(new_values[0], "tp", axis=2, tiled=True),
    )
    owners = page_owner[0]
    fill_counts = page_fill[0]
    slot_targets = target_slot[0]
    clipped = jnp.clip(owners, 0, row_count - 1)
    page_target = jnp.take(slot_targets, clipped)
    occupied = owners < row_count
    moving = occupied & (page_target < row_count)
    partner_targets = swapped(slot_targets, "group", partner_bit)
    slot_ids = lax.broadcasted_iota(jnp.int32, (row_count,), 0)
    mover_ids = lax.broadcasted_iota(jnp.int32, (MOVE, row_count), 0)
    their_moving = partner_targets < row_count
    their_rank = jnp.cumsum(their_moving.astype(jnp.int32)) - 1
    their_pick = their_moving[None, :] & (their_rank[None, :] == mover_ids)
    pick_rows = jnp.sum(their_pick.astype(jnp.int32) * partner_targets[None, :], axis=1)
    pick_valid = jnp.any(their_pick, axis=1)
    send_pick = pick_valid[:, None] & (pick_rows[:, None] == slot_ids[None, :])
    sent_queries = jnp.einsum(
        "mr,rsd->msd",
        send_pick.astype(jnp.bfloat16),
        query_rows,
        preferred_element_type=jnp.float32,
    ).astype(jnp.bfloat16)
    arrived_queries = swapped(sent_queries, "group", partner_bit)
    own_moving = slot_targets < row_count
    own_rank = jnp.cumsum(own_moving.astype(jnp.int32)) - 1
    page_rank = jnp.take(own_rank, clipped)
    local_rows = jnp.where(
        occupied, jnp.where(moving, row_count + page_rank, owners), row_count + MOVE
    )
    joined = page_states(
        jnp.concatenate([query_rows, arrived_queries], axis=0),
        key_pages[0],
        value_pages[0],
        local_rows,
        fill_counts,
        row_count + MOVE,
    )
    own_part = tuple((member_array[:row_count] for member_array in joined))
    theirs = tuple((member_array[row_count:] for member_array in joined))
    returned = swapped((theirs[0], theirs[1], theirs[2]), "group", partner_bit)
    placement_table = send_pick.astype(jnp.float32)
    placed_any = jnp.any(send_pick, axis=0)
    placed_max = jnp.where(
        placed_any[:, None, None],
        jnp.einsum("mr,msh->rsh", placement_table, returned[0], precision=lax.Precision.HIGHEST),
        neg_big,
    )
    placed_sum = jnp.einsum(
        "mr,msh->rsh", placement_table, returned[1], precision=lax.Precision.HIGHEST
    )
    placed_acc = jnp.einsum(
        "mr,mshd->rshd", placement_table, returned[2], precision=lax.Precision.HIGHEST
    )
    states = merge_states(own_part, (placed_max, placed_sum, placed_acc))
    head_kv_all = lax.broadcasted_iota(jnp.int32, (HEADS,), 0) // (HEADS // KVH)
    query_heads = query_rows.reshape(row_count, step_count, HEADS, HD)
    combined = combined_all((states[0], states[1], states[2]), "tp", merge_states)
    new_terms = new_token_states(query_heads, key_rows, value_rows, head_kv_all)
    finished = merge_states(combined, new_terms)
    attention = (
        (finished[2] / finished[1][..., None])
        .astype(jnp.bfloat16)
        .reshape(row_count * step_count, HEADS * HD)
    )
    projected = jnp.dot(attention, out_weight, preferred_element_type=jnp.float32).astype(
        jnp.bfloat16
    )
    return projected.reshape(1, row_count, step_count, out_weight.shape[1])


def solution(mesh):
    placed = (
        P("group", None, None, "tp"),
        P("group", None, None, "tp"),
        P("group", None, None, "tp"),
        P("group", "tp", None, None),
        P("group", "tp", None, None),
        P("group", "tp"),
        P("group", "tp"),
        P("group", None),
        P(None, "tp"),
    )
    return jax.shard_map(
        per_device,
        mesh=mesh,
        in_specs=placed,
        out_specs=P("group", None, None, "tp"),
        check_vma=False,
    )
```

profile of v0, /device:TPU:0, one launch (start us, length us, event | category | flops | bytes accessed | tf_op | source)
XLA Modules:
  0.0 223.7 jit_solution(14644763378011074717)
XLA Ops:
  6.5 3.0 %collective-permute-start = (s32[8]{0:T(128)}, s32[8]{0:T(128)S(1)}, u32[]{:S(2)}, u32[]{:S(2)}) collective-permute-start(s32[8]{0:T(128)} %bitcast.168), channel_id=1, source_target_pairs={{0,16},{16,0},{1,17},{17,1},{2,18},{18,2},{3,19},{19,3},{4,20},{20... | collective-permute-start | bytes 104 | tf_op jit(solution)/shard_map/ppermute | solution.py:16
  9.5 0.7 fusion.42
  10.2 1.6 fusion.52
  12.7 10.6 %broadcast_compare_fusion = (pred[64]{0:T(512)(128)(4,1)S(1)}, s32[64]{0:T(128)S(1)}) fusion(s32[]{:T(128)} %bitcast.22, s32[]{:T(128)} %bitcast.21, s32[]{:T(128)} %bitcast.20, s32[]{:T(128)} %bitcast.19, s32[]{:T(128)} %bitcast.18, s32[]{:T(128)} %bitcast.17, s32[]{:T(128)} %bitcast.16, s32[]{:T(128)} %bitcast.15, s32[]{:T(128)} %bitcast.12, s32[]{:T(128)} %bitcast.11, ...), kind=kLoop, calls=%fused_computation.120 | loop fusion | flops 2368 | bytes 640 | tf_op jit(solution)/shard_map/lt | solution.py:56
  23.4 22.6 %all-gather = bf16[1,8,2,8192]{3,2,1,0:T(2,128)(2,1)S(1)} all-gather(bf16[1,8,2,512]{3,2,1,0:T(2,128)(2,1)} %param.15), channel_id=2, replica_groups=mesh['group'=2,'tp'=16] {'tp'}, dimensions={3}, use_global_device_ids=true | all-gather | bytes 278528 | tf_op jit(solution)/shard_map/all_gather | solution.py:125
  45.9 2.4 %copy.149 = bf16[128,8,8,128]{3,2,1,0:T(8,128)(2,1)S(1)} copy(bf16[128,8,8,128]{3,1,2,0:T(8,128)(2,1)} %bitcast.155) | data formatting | bytes 4194304
  48.3 1.5 bitcast_bitcast_fusion.1
  50.4 1.5 bitcast_bitcast_fusion
  52.2 0.7 select_reduce_fusion.1
  53.6 1.3 compare_and_fusion.2
  55.9 1.3 fusion.43
  57.3 2.1 collective-permute-done.1
  59.7 6.1 %gather_fusion = bf16[64,2,8192]{2,1,0:T(2,128)(2,1)S(1)} fusion(bf16[9,2,8192]{2,1,0:T(2,128)(2,1)S(1)} %pad_maximum_fusion, s32[1024]{0:T(1024)S(1)} %pad_clamp_fusion.1), kind=kCustom, calls=%fused_computation.2 | custom fusion | bytes 4194560 | tf_op jit(solution)/shard_map/jit(_take)/gather | solution.py:47
  65.8 2.9 %gather.19 = bf16[64,2,8,8,128]{4,3,2,1,0:T(8,128)(2,1)} reshape(bf16[64,2,8192]{2,1,0:T(2,128)(2,1)S(1)} %gather_fusion) | data formatting | bytes 4194304 | tf_op jit(solution)/shard_map/jit(_take)/gather | solution.py:47
  68.7 5.8 %bitcast_reduce_fusion = (f32[64,2,8,8]{3,1,2,0:T(2,128)S(1)}, f32[64,8,2,8,16]{4,3,2,1,0:T(8,128)}) fusion(pred[64,16]{1,0:T(8,128)(4,1)S(1)} %fusion.29, bf16[64,16,8,128,1]{3,2,1,0,4:T(8,128)(2,1)} %bitcast_bitcast_fusion.1, bf16[64,2,8,8,128]{4,3,2,1,0:T(8,128)(2,1)} %gather.19, pred[64]{0:T(512)(128)(4,1)S(1)} %get-tuple-element.215), kind=kOutput, calls=%fused_computation.16 | convolution fusion | flops 34988032 | bytes 4752448 | tf_op jit(solution)/shard_map/psgjd,ptgd->psgjt/dot_general | solution.py:53
  76.8 4.9 %convert_reduce_fusion = f32[64,2,8,8]{3,1,2,0:T(2,128)S(1)} fusion(f32[64,2,8,8]{3,1,2,0:T(2,128)S(1)} %copy.112, f32[64,8,2,8,16]{4,3,2,1,0:T(8,128)} %get-tuple-element.238, pred[64,16]{1,0:T(8,128)(4,1)S(1)} %fusion.29), kind=kLoop, calls=%fused_computation.20 | loop fusion | flops 909312 | bytes 590848 | tf_op jit(solution)/shard_map/reduce_sum | solution.py:71
  82.3 1.5 collective-permute-start.3
  83.8 4.2 %convolution_bitcast_fusion = f32[64,2,8,8,128]{4,3,1,2,0:T(8,128)S(1)} fusion(bf16[64,16,8,128,1]{3,2,1,0,4:T(8,128)(2,1)S(1)} %copy-done.1, f32[64,8,2,8,16]{4,3,2,1,0:T(8,128)} %get-tuple-element.238, f32[64,2,8,8]{3,1,2,0:T(2,128)S(1)} %copy.112, pred[64,16]{1,0:T(8,128)(4,1)S(1)} %fusion.29), kind=kOutput, calls=%fused_computation.22 | convolution fusion | flops 34209792 | bytes 6849536 | tf_op jit(solution)/shard_map/psgjt,ptgd->psgjd/dot_general | solution.py:68
  88.6 3.8 %fusion.3 = f32[9,16384]{1,0:T(8,128)S(1)} fusion(f32[8,8,128,128]{3,2,1,0:T(8,128)S(1)} %bitcast.149, s32[64]{0:T(128)S(1)} %get-tuple-element.214), kind=kOutput, calls=%fused_computation.12 | convolution fusion | flops 113246784 | bytes 4784384 | tf_op jit(solution)/shard_map/dot_general | solution.py:76
  93.3 3.6 %collective-permute-done.4 = f32[1,2,64,128]{3,2,1,0:T(8,128)S(1)} collective-permute-done((f32[1,2,64,128]{3,2,1,0:T(8,128)S(1)}, f32[1,2,64,128]{3,2,1,0:T(8,128)S(1)}, u32[]{:S(2)}, u32[]{:S(2)}) %collective-permute-start.4) | collective-permute-done | bytes 65568 | tf_op jit(solution)/shard_map/ppermute | solution.py:16
  96.9 1.2 fusion.19
  98.4 20.6 %all-gather.5 = bf16[1,8,2,1024]{1,2,0,3:T(2,128)(2,1)S(1)} all-gather(bf16[1,8,2,64]{1,2,0,3:T(2,128)(2,1)S(1)} %copy.125), channel_id=7, replica_groups=mesh['group'=2,'tp'=16] {'tp'}, dimensions={3}, use_global_device_ids=true | all-gather | bytes 34816 | tf_op jit(solution)/shard_map/all_gather | solution.py:127
  119.3 22.3 %all-gather.4 = bf16[1,8,2,1024]{1,2,0,3:T(2,128)(2,1)S(1)} all-gather(bf16[1,8,2,64]{1,2,0,3:T(2,128)(2,1)S(1)} %copy.117), channel_id=6, replica_groups=mesh['group'=2,'tp'=16] {'tp'}, dimensions={3}, use_global_device_ids=true | all-gather | bytes 34816 | tf_op jit(solution)/shard_map/all_gather | solution.py:126
  141.9 0.7 gather_fusion.3
  142.6 0.7 gather_fusion.2
  143.5 1.1 fusion.54
  144.7 0.9 fusion.30
  145.8 2.4 %fusion.24 = f32[8,64,128,2]{2,3,1,0:T(2,128)S(1)} fusion(bf16[8,2,64,128]{3,0,1,2:T(8,128)(2,1)S(1)} %get-tuple-element.234, f32[8,2,64,2]{1,3,2,0:T(2,128)S(1)} %get-tuple-element.236, pred[2,2]{0,1:T(4,128)(4,1)S(1)} %iota_compare_fusion.4, f32[8,2,64]{1,2,0:T(8,128)S(1)} %get-tuple-element.235), kind=kOutput, calls=%fused_computation.50 | convolution fusion | flops 3149824 | bytes 798724 | tf_op jit(solution)/shard_map/rshu,ruhd->rshd/dot_general | solution.py:106
  148.2 18.7 %all-gather.2 = f32[128,2,64]{2,1,0:T(2,128)S(1)} all-gather(f32[8,2,64]{2,1,0:T(2,128)S(1)} %get-tuple-element.209), channel_id=4, replica_groups=mesh['group'=2,'tp'=16] {'tp'}, dimensions={0}, use_global_device_ids=true | all-gather | bytes 69632 | tf_op jit(solution)/shard_map/all_gather | solution.py:20
  166.8 19.0 %all-gather.1 = f32[128,2,64]{2,1,0:T(2,128)S(1)} all-gather(f32[8,2,64]{2,1,0:T(2,128)S(1)} %get-tuple-element.212), channel_id=3, replica_groups=mesh['group'=2,'tp'=16] {'tp'}, dimensions={0}, use_global_device_ids=true | all-gather | bytes 69632 | tf_op jit(solution)/shard_map/all_gather | solution.py:20
  185.8 1.1 slice.104
  186.9 24.2 %while.19 = (s32[]{:T(128)}, f32[8,2,64]{2,1,0:T(2,128)S(1)}, f32[8,2,64]{2,1,0:T(2,128)S(1)}, f32[8,2,64,128]{3,2,1,0:T(8,128)S(1)}, f32[16,8,2,64]{3,2,1,0:T(2...) while((s32[]{:T(128)}, f32[8,2,64]{2,1,0:T(2,128)S(1)}, ...), condition=%wide.region_8.10_spmd, body=%wide.region_7.9_spmd.sunk | while | flops 399365 | bytes 1613967 | solution.py:25
  187.0 1.5 fusion.60
  188.6 1.5 fusion.60
  190.2 1.5 fusion.60
  191.8 1.5 fusion.60
  193.4 1.5 fusion.60
  195.0 1.5 fusion.60
  196.6 1.5 fusion.60
  198.2 1.5 fusion.60
  199.9 1.5 fusion.60
  201.5 1.5 fusion.60
  203.1 1.5 fusion.60
  204.7 1.5 fusion.60
  206.3 1.5 fusion.60
  207.9 1.5 fusion.60
  209.5 1.5 fusion.60
  211.6 4.6 %convolution_convert_fusion = bf16[16,512]{1,0:T(8,128)(2,1)S(1)} fusion(bf16[8192,512]{1,0:T(8,128)(2,1)} %param.23, bf16[2,8,64,128]{3,2,1,0:T(8,128)(2,1)S(1)} %bitcast.154), kind=kOutput, calls=%fused_computation.33 | convolution fusion | flops 134225920 | bytes 8667136 | tf_op jit(solution)/shard_map/dot_general | solution.py:193
  (88 shorter events, 11.2 us)
Async XLA Ops:
  6.5 179.3 %all-gather.8.cloned.1.call-start = ((), (), s32[]{:S(2)}) async-start(), calls=%async_computation | async-start | bytes 8912896 | tf_op jit(solution)/shard_map/all_gather | solution.py:20
  6.5 45.5 %collective-permute-start = (s32[8]{0:T(128)}, s32[8]{0:T(128)S(1)}, u32[]{:S(2)}, u32[]{:S(2)}) collective-permute-start(s32[8]{0:T(128)} %bitcast.168), channel_id=1, source_target_pairs={{0,16},{16,0},{1,17},{17,1},{2,18},{18,2},{3,19},{19,3},{4,20},{20... | collective-permute-start | bytes 104 | tf_op jit(solution)/shard_map/ppermute | solution.py:16
  45.9 3.9 %copy-start = (bf16[1,64,16,1024]{3,2,1,0:T(8,128)(2,1)S(1)}, bf16[1,64,16,1024]{3,2,1,0:T(8,128)(2,1)}, u32[]{:S(2)}) copy-start(bf16[1,64,16,1024]{3,2,1,0:T(8,128)(2,1)} %param.19) | copy-start | bytes 6291460
  49.8 2.1 copy-start.4
  55.4 4.0 %collective-permute-start.1 = (bf16[1,2,8192]{2,1,0:T(2,128)(2,1)S(1)}, bf16[1,2,8192]{2,1,0:T(2,128)(2,1)S(1)}, u32[]{:S(2)}, u32[]{:S(2)}) collective-permute-start(bf16[1,2,8192]{2,1,0:T(2,128)(2,1)S(1)} %copy.193), channel_id=1, source_target_pairs={{0,16},{16,0},{1,17},{17,1},{2,18},{18,2},{3,19},{19,3},{4,20},{20... | collective-permute-start | bytes 98312 | tf_op jit(solution)/shard_map/ppermute | solution.py:16
  74.5 9.3 %copy-start.1 = (bf16[64,16,8,128,1]{3,2,1,0,4:T(8,128)(2,1)S(1)}, bf16[64,16,8,128,1]{3,2,1,0,4:T(8,128)(2,1)}, u32[]{:S(2)}) copy-start(bf16[64,16,8,128,1]{3,2,1,0,4:T(8,128)(2,1)} %bitcast_bitcast_fusion) | copy-start | bytes 6291460
  75.7 17.5 %collective-permute-start.2 = (f32[1,2,64]{2,1,0:T(2,128)S(1)}, f32[1,2,64]{2,1,0:T(2,128)S(1)}, u32[]{:S(2)}, u32[]{:S(2)}) collective-permute-start(f32[1,2,64]{2,1,0:T(2,128)S(1)} %slice.42), channel_id=1, source_target_pairs={{0,16},{16,0},{1,17},{17,1},{2,18},{18,2},{3,19},{19,3},{4,20},{20... | collective-permute-start | bytes 1544 | tf_op jit(solution)/shard_map/ppermute | solution.py:16
  82.3 10.9 %collective-permute-start.3 = (f32[1,2,64]{2,1,0:T(2,128)S(1)}, f32[1,2,64]{2,1,0:T(2,128)S(1)}, u32[]{:S(2)}, u32[]{:S(2)}) collective-permute-start(f32[1,2,64]{2,1,0:T(2,128)S(1)} %slice.46), channel_id=1, source_target_pairs={{0,16},{16,0},{1,17},{17,1},{2,18},{18,2},{3,19},{19,3},{4,20},{20... | collective-permute-start | bytes 1544 | tf_op jit(solution)/shard_map/ppermute | solution.py:16
  88.6 9.6 %copy-start.2 = (bf16[1,8,2,64]{3,2,1,0:T(2,128)(2,1)S(1)}, bf16[1,8,2,64]{3,2,1,0:T(2,128)(2,1)}, u32[]{:S(2)}) copy-start(bf16[1,8,2,64]{3,2,1,0:T(2,128)(2,1)} %param.16) | copy-start | bytes 6148
  88.6 9.7 %copy-start.3 = (bf16[1,8,2,64]{3,2,1,0:T(2,128)(2,1)S(1)}, bf16[1,8,2,64]{3,2,1,0:T(2,128)(2,1)}, u32[]{:S(2)}) copy-start(bf16[1,8,2,64]{3,2,1,0:T(2,128)(2,1)} %param.17) | copy-start | bytes 6148
  92.7 4.3 %collective-permute-start.4 = (f32[1,2,64,128]{3,2,1,0:T(8,128)S(1)}, f32[1,2,64,128]{3,2,1,0:T(8,128)S(1)}, u32[]{:S(2)}, u32[]{:S(2)}) collective-permute-start(f32[1,2,64,128]{3,2,1,0:T(8,128)S(1)} %bitcast.167), channel_id=1, source_target_pairs={{0,16},{16,0},{1,17},{17,1},{2,18},{18,2},{3,19},{19,3},{4,20},{20... | collective-permute-start | bytes 196616 | tf_op jit(solution)/shard_map/ppermute | solution.py:16
Sparse Core Ops, SparseCore 0:
  98.3 73.7 all-gather.7
where the time goes:
time: 225 us; the launch traced here: 224 us
  blocking collectives  103 us (46%)
  other arithmetic  48 us (21%)
  local copies, waits for them, and re-layouts  24.3 us (11%)
  matrix products  22.4 us (10%)
  between operations  13.8 us (6%)
  starting transfers between devices  6.16 us (3%)
  waiting for transfers between devices  5.69 us (3%)
    all_gather x2, blocking collectives, combined_all(): gathered = jax.tree.map(lambda a: lax.all_gather(a, axis), part)  37.6 us
    add x16, other arithmetic, merge_states(): first[2] * scale_first[..., None] + second[2] * scale_second[..., None]  24.4 us
    all_gather x1, blocking collectives, per_device(): lax.all_gather(queries[0], 'tp', axis=2, tiled=True)  22.6 us
    all_gather x1, blocking collectives, per_device(): lax.all_gather(new_keys[0], 'tp', axis=2, tiled=True)  22.3 us
    all_gather x1, blocking collectives, per_device(): lax.all_gather(new_values[0], 'tp', axis=2, tiled=True)  20.6 us
    lt x1, other arithmetic, page_states(): owner_rows < row_count  10.6 us
    gather x2, local copies, waits for them, and re-layouts, page_states(): jnp.take(query_rows, clipped, axis=0)  8.94 us
    ppermute x5, starting transfers between devices, swapped(): lax.ppermute(value, axis, [(i, i ^ 1 << distance) for i in range(lax.axis...  6.16 us
  transfers between devices with their start and end apart: 6, of which 2 were waited for; matrix products, arithmetic and copies ran while one was open for 19% of the time, Pallas kernels for 0%

commit v1 on v0

--- a/solution.py
+++ b/solution.py
@@ -10,6 +10,12 @@
 PAGE = 16
 MOVE = 1
 neg_big = -1e30
+
+
+def stack_and_merge(x, axis, along):
+    parts = lax.all_gather(x, axis, axis=0, tiled=False)
+    whole = jnp.concatenate(parts, axis=along)
+    return whole
 
 
 def swapped(value, axis, distance):
@@ -122,7 +128,7 @@
     step_count = queries.shape[2]
     partner_bit = lax.axis_size("group").bit_length() - 2
     query_rows, key_rows, value_rows = (
-        lax.all_gather(queries[0], "tp", axis=2, tiled=True),
+        stack_and_merge(queries[0], "tp", 2),
         lax.all_gather(new_keys[0], "tp", axis=2, tiled=True),
         lax.all_gather(new_values[0], "tp", axis=2, tiled=True),
     )

time: 225 us -> 228 us (1.013)
  transfers between devices with their start and end apart: 6 -> 6, of which waited for: 2 -> 2; matrix products, arithmetic and copies ran while one was open for 19% -> 20% of each run, Pallas kernels for 0% -> 0%
where the time goes in v1:
time: 228 us; the launch traced here: 226 us
  blocking collectives  103 us (45%)
  other arithmetic  47.9 us (21%)
  local copies, waits for them, and re-layouts  25.6 us (11%)
  matrix products  23.5 us (10%)
  between operations  13.8 us (6%)
  starting transfers between devices  6.16 us (3%)
  waiting for transfers between devices  5.69 us (2%)
    all_gather x2, blocking collectives, combined_all(): gathered = jax.tree.map(lambda a: lax.all_gather(a, axis), part)  37.7 us
    add x16, other arithmetic, merge_states(): first[2] * scale_first[..., None] + second[2] * scale_second[..., None]  24.4 us
    all_gather x1, blocking collectives, per_device(): lax.all_gather(new_keys[0], 'tp', axis=2, tiled=True)  22.5 us
    all_gather x1, blocking collectives, stack_and_merge(): parts = lax.all_gather(x, axis, axis=0, tiled=False)  22.3 us
    all_gather x1, blocking collectives, per_device(): lax.all_gather(new_values[0], 'tp', axis=2, tiled=True)  20.6 us
    lt x1, other arithmetic, page_states(): owner_rows < row_count  10.6 us
    gather x2, local copies, waits for them, and re-layouts, page_states(): jnp.take(query_rows, clipped, axis=0)  8.94 us
    ppermute x5, starting transfers between devices, swapped(): lax.ppermute(value, axis, [(i, i ^ 1 << distance) for i in range(lax.axis...  6.16 us
  transfers between devices with their start and end apart: 6, of which 2 were waited for; matrix products, arithmetic and copies ran while one was open for 20% of the time, Pallas kernels for 0%

profile of v1, /device:TPU:0, one launch (start us, length us, event | category | flops | bytes accessed | tf_op | source)
XLA Modules:
  0.0 226.2 jit_solution(15470466513637657264)
XLA Ops:
  6.5 3.0 %collective-permute-start = (s32[8]{0:T(128)}, s32[8]{0:T(128)S(1)}, u32[]{:S(2)}, u32[]{:S(2)}) collective-permute-start(s32[8]{0:T(128)} %bitcast.171), channel_id=1, source_target_pairs={{0,16},{16,0},{1,17},{17,1},{2,18},{18,2},{3,19},{19,3},{4,20},{20... | collective-permute-start | bytes 104 | tf_op jit(solution)/shard_map/ppermute | solution.py:22
  9.5 0.7 fusion.40
  10.2 1.6 fusion.48
  12.7 10.6 %broadcast_compare_fusion = (pred[64]{0:T(512)(128)(4,1)S(1)}, s32[64]{0:T(128)S(1)}) fusion(s32[]{:T(128)} %bitcast.22, s32[]{:T(128)} %bitcast.21, s32[]{:T(128)} %bitcast.20, s32[]{:T(128)} %bitcast.19, s32[]{:T(128)} %bitcast.18, s32[]{:T(128)} %bitcast.17, s32[]{:T(128)} %bitcast.16, s32[]{:T(128)} %bitcast.15, s32[]{:T(128)} %bitcast.12, s32[]{:T(128)} %bitcast.11, ...), kind=kLoop, calls=%fused_computation.118 | loop fusion | flops 2368 | bytes 640 | tf_op jit(solution)/shard_map/lt | solution.py:62
  23.4 0.7 copy.126
  24.1 22.3 %all_gather.27 = bf16[16,8,2,512]{3,1,2,0:T(8,128)(2,1)S(1)} all-gather(bf16[1,8,2,512]{3,1,2,0:T(8,128)(2,1)S(1)} %copy.126), channel_id=1, replica_groups=mesh['group'=2,'tp'=16] {'tp'}, dimensions={0}, use_global_device_ids=true | all-gather | bytes 278528 | tf_op jit(solution)/shard_map/all_gather | solution.py:16
  46.7 2.4 %copy.175 = bf16[128,8,8,128]{3,2,1,0:T(8,128)(2,1)S(1)} copy(bf16[128,8,8,128]{3,1,2,0:T(8,128)(2,1)} %bitcast.158) | data formatting | bytes 4194304
  49.1 1.5 bitcast_bitcast_fusion.1
  51.2 1.5 bitcast_bitcast_fusion
  53.0 0.7 select_reduce_fusion.1
  54.3 1.3 bitcast_convert_fusion.1
  55.7 1.5 fusion.35
  57.9 1.3 compare_and_fusion.2
  59.2 2.1 collective-permute-done.1
  61.7 6.1 %gather_fusion = bf16[64,2,8192]{2,1,0:T(2,128)(2,1)S(1)} fusion(bf16[9,2,8192]{2,1,0:T(2,128)(2,1)S(1)} %pad_maximum_fusion, s32[1024]{0:T(1024)S(1)} %pad_clamp_fusion.1), kind=kCustom, calls=%fused_computation.2 | custom fusion | bytes 4194560 | tf_op jit(solution)/shard_map/jit(_take)/gather | solution.py:53
  67.8 2.9 %reshape.376 = bf16[64,2,8,8,128]{4,3,2,1,0:T(8,128)(2,1)} reshape(bf16[64,2,8192]{2,1,0:T(2,128)(2,1)S(1)} %gather_fusion) | data formatting | bytes 4194304 | tf_op jit(solution)/shard_map/jit(_take)/gather | solution.py:53
  70.6 5.7 %bitcast_reduce_fusion = (f32[64,2,8,8]{3,1,2,0:T(2,128)S(1)}, f32[64,8,2,8,16]{4,3,2,1,0:T(8,128)}) fusion(pred[64,16]{1,0:T(8,128)(4,1)S(1)} %fusion.26, bf16[64,16,8,128,1]{3,2,1,0,4:T(8,128)(2,1)} %bitcast_bitcast_fusion.1, bf16[64,2,8,8,128]{4,3,2,1,0:T(8,128)(2,1)} %reshape.376, pred[64]{0:T(512)(128)(4,1)S(1)} %get-tuple-element.215), kind=kOutput, calls=%fused_computation.16 | convolution fusion | flops 34988032 | bytes 4752448 | tf_op jit(solution)/shard_map/psgjd,ptgd->psgjt/dot_general | solution.py:59
  78.7 4.9 %convert_reduce_fusion = f32[64,2,8,8]{3,1,2,0:T(2,128)S(1)} fusion(f32[64,2,8,8]{3,1,2,0:T(2,128)S(1)} %copy.135, f32[64,8,2,8,16]{4,3,2,1,0:T(8,128)} %get-tuple-element.238, pred[64,16]{1,0:T(8,128)(4,1)S(1)} %fusion.26), kind=kLoop, calls=%fused_computation.20 | loop fusion | flops 909312 | bytes 590848 | tf_op jit(solution)/shard_map/reduce_sum | solution.py:77
  84.2 1.5 collective-permute-start.3
  85.7 4.2 %convolution_bitcast_fusion = f32[64,2,8,8,128]{4,3,1,2,0:T(8,128)S(1)} fusion(bf16[64,16,8,128,1]{3,2,1,0,4:T(8,128)(2,1)S(1)} %copy-done.1, f32[64,8,2,8,16]{4,3,2,1,0:T(8,128)} %get-tuple-element.238, f32[64,2,8,8]{3,1,2,0:T(2,128)S(1)} %copy.135, pred[64,16]{1,0:T(8,128)(4,1)S(1)} %fusion.26), kind=kOutput, calls=%fused_computation.22 | convolution fusion | flops 34209792 | bytes 6849536 | tf_op jit(solution)/shard_map/psgjt,ptgd->psgjd/dot_general | solution.py:74
  90.4 3.8 %fusion.3 = f32[9,16384]{1,0:T(8,128)S(1)} fusion(f32[8,8,128,128]{3,2,1,0:T(8,128)S(1)} %bitcast.150, s32[64]{0:T(128)S(1)} %get-tuple-element.214), kind=kOutput, calls=%fused_computation.12 | convolution fusion | flops 113246784 | bytes 4784384 | tf_op jit(solution)/shard_map/dot_general | solution.py:82
  95.2 3.6 %collective-permute-done.4 = f32[1,2,64,128]{3,2,1,0:T(8,128)S(1)} collective-permute-done((f32[1,2,64,128]{3,2,1,0:T(8,128)S(1)}, f32[1,2,64,128]{3,2,1,0:T(8,128)S(1)}, u32[]{:S(2)}, u32[]{:S(2)}) %collective-permute-start.4) | collective-permute-done | bytes 65568 | tf_op jit(solution)/shard_map/ppermute | solution.py:22
  98.8 1.2 fusion.18
  100.6 20.6 %all-gather.4 = bf16[1,8,2,1024]{1,2,0,3:T(2,128)(2,1)S(1)} all-gather(bf16[1,8,2,64]{1,2,0,3:T(2,128)(2,1)S(1)} %copy.150), channel_id=6, replica_groups=mesh['group'=2,'tp'=16] {'tp'}, dimensions={3}, use_global_device_ids=true | all-gather | bytes 34816 | tf_op jit(solution)/shard_map/all_gather | solution.py:133
  121.5 22.5 %all-gather.3 = bf16[1,8,2,1024]{1,2,0,3:T(2,128)(2,1)S(1)} all-gather(bf16[1,8,2,64]{1,2,0,3:T(2,128)(2,1)S(1)} %copy.140), channel_id=5, replica_groups=mesh['group'=2,'tp'=16] {'tp'}, dimensions={3}, use_global_device_ids=true | all-gather | bytes 34816 | tf_op jit(solution)/shard_map/all_gather | solution.py:132
  145.9 1.1 fusion.50
  147.1 0.9 fusion.27
  148.2 2.4 %fusion.21 = f32[8,64,128,2]{2,3,1,0:T(2,128)S(1)} fusion(bf16[8,2,64,128]{3,0,1,2:T(8,128)(2,1)S(1)} %get-tuple-element.234, f32[8,2,64,2]{1,3,2,0:T(2,128)S(1)} %get-tuple-element.236, pred[2,2]{0,1:T(4,128)(4,1)S(1)} %iota_compare_fusion.4, f32[8,2,64]{1,2,0:T(8,128)S(1)} %get-tuple-element.235), kind=kOutput, calls=%fused_computation.47 | convolution fusion | flops 3149824 | bytes 798724 | tf_op jit(solution)/shard_map/rshu,ruhd->rshd/dot_general | solution.py:112
  150.6 18.7 %all-gather.1 = f32[128,2,64]{2,1,0:T(2,128)S(1)} all-gather(f32[8,2,64]{2,1,0:T(2,128)S(1)} %get-tuple-element.209), channel_id=3, replica_groups=mesh['group'=2,'tp'=16] {'tp'}, dimensions={0}, use_global_device_ids=true | all-gather | bytes 69632 | tf_op jit(solution)/shard_map/all_gather | solution.py:26
  169.3 19.0 %all-gather = f32[128,2,64]{2,1,0:T(2,128)S(1)} all-gather(f32[8,2,64]{2,1,0:T(2,128)S(1)} %get-tuple-element.212), channel_id=2, replica_groups=mesh['group'=2,'tp'=16] {'tp'}, dimensions={0}, use_global_device_ids=true | all-gather | bytes 69632 | tf_op jit(solution)/shard_map/all_gather | solution.py:26
  188.3 1.1 slice.104
  189.4 24.1 %while.19 = (s32[]{:T(128)}, f32[8,2,64]{2,1,0:T(2,128)S(1)}, f32[8,2,64]{2,1,0:T(2,128)S(1)}, f32[8,2,64,128]{3,2,1,0:T(8,128)S(1)}, f32[16,8,2,64]{3,2,1,0:T(2...) while((s32[]{:T(128)}, f32[8,2,64]{2,1,0:T(2,128)S(1)}, ...), condition=%wide.region_8.10_spmd, body=%wide.region_7.9_spmd.sunk | while | flops 399365 | bytes 1613967 | solution.py:31
  189.5 1.5 fusion.57
  191.1 1.5 fusion.57
  192.7 1.5 fusion.57
  194.3 1.5 fusion.57
  195.9 1.5 fusion.57
  197.5 1.5 fusion.57
  199.1 1.5 fusion.57
  200.7 1.5 fusion.57
  202.4 1.5 fusion.57
  204.0 1.5 fusion.57
  205.6 1.5 fusion.57
  207.2 1.5 fusion.57
  208.8 1.5 fusion.57
  210.4 1.5 fusion.57
  212.0 1.5 fusion.57
  214.1 4.6 %convolution_convert_fusion = bf16[16,512]{1,0:T(8,128)(2,1)S(1)} fusion(bf16[8192,512]{1,0:T(8,128)(2,1)} %param.23, bf16[2,8,64,128]{3,2,1,0:T(8,128)(2,1)S(1)} %bitcast.157), kind=kOutput, calls=%fused_computation.33 | convolution fusion | flops 134225920 | bytes 8667136 | tf_op jit(solution)/shard_map/dot_general | solution.py:199
  (93 shorter events, 12.8 us)
Async XLA Ops:
  6.5 181.8 %all-gather.7.cloned.1.call-start = ((), (), s32[]{:S(2)}) async-start(), calls=%async_computation | async-start | bytes 8912896 | tf_op jit(solution)/shard_map/all_gather | solution.py:26
  6.5 46.2 %collective-permute-start = (s32[8]{0:T(128)}, s32[8]{0:T(128)S(1)}, u32[]{:S(2)}, u32[]{:S(2)}) collective-permute-start(s32[8]{0:T(128)} %bitcast.171), channel_id=1, source_target_pairs={{0,16},{16,0},{1,17},{17,1},{2,18},{18,2},{3,19},{19,3},{4,20},{20... | collective-permute-start | bytes 104 | tf_op jit(solution)/shard_map/ppermute | solution.py:22
  46.7 3.9 %copy-start = (bf16[1,64,16,1024]{3,2,1,0:T(8,128)(2,1)S(1)}, bf16[1,64,16,1024]{3,2,1,0:T(8,128)(2,1)}, u32[]{:S(2)}) copy-start(bf16[1,64,16,1024]{3,2,1,0:T(8,128)(2,1)} %param.19) | copy-start | bytes 6291460
  50.6 2.1 copy-start.4
  57.3 4.0 %collective-permute-start.1 = (bf16[1,2,8192]{2,1,0:T(2,128)(2,1)S(1)}, bf16[1,2,8192]{2,1,0:T(2,128)(2,1)S(1)}, u32[]{:S(2)}, u32[]{:S(2)}) collective-permute-start(bf16[1,2,8192]{2,1,0:T(2,128)(2,1)S(1)} %copy.224), channel_id=1, source_target_pairs={{0,16},{16,0},{1,17},{17,1},{2,18},{18,2},{3,19},{19,3},{4,20},{20... | collective-permute-start | bytes 98312 | tf_op jit(solution)/shard_map/ppermute | solution.py:22
  76.4 9.3 %copy-start.1 = (bf16[64,16,8,128,1]{3,2,1,0,4:T(8,128)(2,1)S(1)}, bf16[64,16,8,128,1]{3,2,1,0,4:T(8,128)(2,1)}, u32[]{:S(2)}) copy-start(bf16[64,16,8,128,1]{3,2,1,0,4:T(8,128)(2,1)} %bitcast_bitcast_fusion) | copy-start | bytes 6291460
  77.6 17.5 %collective-permute-start.2 = (f32[1,2,64]{2,1,0:T(2,128)S(1)}, f32[1,2,64]{2,1,0:T(2,128)S(1)}, u32[]{:S(2)}, u32[]{:S(2)}) collective-permute-start(f32[1,2,64]{2,1,0:T(2,128)S(1)} %slice.42), channel_id=1, source_target_pairs={{0,16},{16,0},{1,17},{17,1},{2,18},{18,2},{3,19},{19,3},{4,20},{20... | collective-permute-start | bytes 1544 | tf_op jit(solution)/shard_map/ppermute | solution.py:22
  84.2 10.9 %collective-permute-start.3 = (f32[1,2,64]{2,1,0:T(2,128)S(1)}, f32[1,2,64]{2,1,0:T(2,128)S(1)}, u32[]{:S(2)}, u32[]{:S(2)}) collective-permute-start(f32[1,2,64]{2,1,0:T(2,128)S(1)} %slice.46), channel_id=1, source_target_pairs={{0,16},{16,0},{1,17},{17,1},{2,18},{18,2},{3,19},{19,3},{4,20},{20... | collective-permute-start | bytes 1544 | tf_op jit(solution)/shard_map/ppermute | solution.py:22
  90.4 9.6 %copy-start.2 = (bf16[1,8,2,64]{3,2,1,0:T(2,128)(2,1)S(1)}, bf16[1,8,2,64]{3,2,1,0:T(2,128)(2,1)}, u32[]{:S(2)}) copy-start(bf16[1,8,2,64]{3,2,1,0:T(2,128)(2,1)} %param.16) | copy-start | bytes 6148
  90.4 9.7 %copy-start.3 = (bf16[1,8,2,64]{3,2,1,0:T(2,128)(2,1)S(1)}, bf16[1,8,2,64]{3,2,1,0:T(2,128)(2,1)}, u32[]{:S(2)}) copy-start(bf16[1,8,2,64]{3,2,1,0:T(2,128)(2,1)} %param.17) | copy-start | bytes 6148
  94.5 4.3 %collective-permute-start.4 = (f32[1,2,64,128]{3,2,1,0:T(8,128)S(1)}, f32[1,2,64,128]{3,2,1,0:T(8,128)S(1)}, u32[]{:S(2)}, u32[]{:S(2)}) collective-permute-start(f32[1,2,64,128]{3,2,1,0:T(8,128)S(1)} %bitcast.170), channel_id=1, source_target_pairs={{0,16},{16,0},{1,17},{17,1},{2,18},{18,2},{3,19},{19,3},{4,20},{20... | collective-permute-start | bytes 196616 | tf_op jit(solution)/shard_map/ppermute | solution.py:22
Sparse Core Ops, SparseCore 0:
  100.1 73.8 all-gather.6
